TPU v7x, 256 devices: a whole 4x4x8 slice. The times are simulated.
256 devices in a mesh: row: 8 (over y, core), col: 32 (over z, x).
Axes of the slice: x: 4, y: 4, z: 8, core: 2. Of those that a mesh axis runs over, the one named last changes fastest.
Arguments:
- factor: float32 [6, 2048, 6, 2048], P(None, 'row', None, 'col'), may hold values from -0.0625 to 0.0625
- diag_inv: float32 [6, 2048, 2048], P(None, None, 'row'), may hold values from -2 to 2, as said below
- structure: int32 [6, 6, 16], P(None, None, 'row'), may hold values 0 or 1
- parent: int32 [6], replicated, may hold values from 1 to 6, as said below
- post: float32 [6, 2048, 64], P(None, 'row', 'col'), may hold values from -6 to 6
Outputs:
- mean_x: float32 [6, 2048, 64], P(None, 'row', 'col')
- variance: float32 [6, 2048], P(None, 'row')
Inputs may be any that keep to these rules, and one draw needn't show every extreme that they name: parent[s] > s for s < 5, and parent[5] = 6; every supernode has at most 2 ancestors, and some supernode has exactly that many. The diagonal of each diag_inv[s] lies in 0.5 to 2.
All inputs are finite; a program needn't handle non-finite values. No bound on the sum of `structure` on one device may be relied on, other than what follows from the above.
Results may differ from a plain program's by a relative error of at most 0.00014.
Values sent between devices are 32-bit elements; how exact they have to be, the bound alone decides.
No kernel may reach another device: no remote copies, remote signals or barrier semaphores. Data moves between devices by JAX's collectives and lax.ppermute only.
A program may use at most 128 MiB of HBM per device.

v0:
```python
import jax
import jax.numpy as jnp
from jax import lax
from jax.sharding import Mesh
from jax.sharding import PartitionSpec as P

LEVELS = 3
COL = ("col_0", "col_1")
HIGHEST = lax.Precision.HIGHEST


def laid_out(parts, dim):
    parts = jnp.moveaxis(parts, 0, dim)
    dims = parts.shape
    return parts.reshape(*dims[:dim], dims[dim] * dims[dim + 1], *dims[dim + 2 :])


def from_everyone(array, axis):
    copies = jnp.broadcast_to(array, (lax.axis_size(axis), *array.shape))
    return lax.all_to_all(copies, axis, split_axis=0, concat_axis=0, tiled=True)


def gathered_copies(array, axis, dim):
    return laid_out(from_everyone(array, axis), dim)


def filled_up(lines, peers):
    spare = -len(lines) % peers
    return jnp.pad(lines, [(0, spare)] + [(0, 0)] * (lines.ndim - 1))


def total_of(array, axis):
    lines = array.reshape(-1, *array.shape[1:][-1:])
    padded = filled_up(lines, lax.axis_size(axis))
    own = lax.psum_scatter(padded, axis, scatter_dimension=0, tiled=True)
    whole = lax.all_gather(own, axis, axis=0, tiled=True)
    return whole[: len(lines)].reshape(array.shape)


def gathered_by_axis(array, axes, dim):
    if not axes:
        return array
    nearer = lax.all_gather(array, axes[-1], axis=dim, tiled=True)
    return gathered_by_axis(nearer, axes[:-1], dim)


def taken_together(array, axis):
    everything = from_everyone(array, axis)
    return jnp.sum(everything, axis=0)


def contract(selected, panel_piece):
    return jnp.einsum("tiw,tin->wn", panel_piece, selected, precision=HIGHEST)


def body(factor, diag_inv, structure, parent, post):
    super_count = factor.shape[0]
    row_width = factor.shape[1]
    col_width = factor.shape[3]
    full_width = diag_inv.shape[1]
    rhs_width = post.shape[2]
    row_at = lax.axis_index("row")
    col_at = lax.axis_index(COL)
    extended = jnp.concatenate([parent, jnp.full((1,), super_count, jnp.int32)])
    slot_ids = jnp.arange(super_count + 1, dtype=jnp.int32)
    targets = jnp.arange(super_count, dtype=jnp.int32)
    ancestor_hops = []
    current = parent
    for hop_index in range(super_count - 1):
        ancestor_hops.append(current)
        onehot = (current[:, None] == slot_ids[None, :]).astype(jnp.int32)
        current = jnp.sum(onehot * extended[None, :], axis=1)
    ancestry = jnp.zeros((super_count, super_count), jnp.float32)
    for hop_targets in ancestor_hops:
        ancestry = ancestry + (hop_targets[:, None] == targets[None, :]).astype(jnp.float32)
    block_rows = row_width // structure.shape[2]
    row_mask = jnp.repeat(structure.astype(jnp.float32), block_rows, axis=2) * ancestry[:, :, None]
    masked = factor * jnp.transpose(row_mask, (1, 2, 0))[:, :, :, None]
    rows_full = jnp.arange(full_width, dtype=jnp.int32)
    own_cols = row_at * row_width + jnp.arange(row_width, dtype=jnp.int32)
    lower_inv = jnp.where((rows_full[:, None] >= own_cols[None, :])[None, :, :], diag_inv, 0.0)
    unit_cols = col_at * col_width + jnp.arange(col_width, dtype=jnp.int32)
    unit_block = (rows_full[:, None] == unit_cols[None, :]).astype(jnp.float32)
    gathered = gathered_copies(post, "row", 1)
    total_cols = super_count * col_width + rhs_width
    solution = jnp.zeros((super_count, row_width, total_cols), jnp.float32)
    for current_sup in range(super_count - 1, -1, -1):
        later_cols = (current_sup + 1) * col_width
        if current_sup == super_count - 1:
            summed = jnp.zeros((full_width, rhs_width), jnp.float32)
        else:
            picks = []
            chosen_rows = []
            for slot_index in range(LEVELS - 1):
                target = ancestor_hops[slot_index][current_sup]
                is_valid = (target < super_count).astype(jnp.float32)
                clamped = jnp.minimum(target, super_count - 1)
                picks.append(
                    lax.dynamic_index_in_dim(
                        masked[:, :, current_sup, :], clamped, 0, keepdims=False
                    )
                    * is_valid
                )
                chosen_rows.append(
                    lax.dynamic_index_in_dim(solution, clamped, 0, keepdims=False)[:, later_cols:]
                )
            blocks = jnp.stack(picks)
            selected = jnp.stack(chosen_rows)
            partial_value = contract(selected, gathered_by_axis(blocks, COL, 2))
            summed = total_of(partial_value, "row")
        split_at = summed.shape[1] - rhs_width
        remaining = jnp.concatenate(
            [-summed[:, :split_at], gathered[current_sup] - summed[:, split_at:]], axis=1
        )
        right = jnp.concatenate([unit_block, remaining], axis=1)
        fresh = jnp.dot(
            lower_inv[current_sup].T, right, precision=HIGHEST, preferred_element_type=jnp.float32
        )
        solution = solution.at[current_sup, :, current_sup * col_width :].set(fresh)
    mean_x = solution[:, :, super_count * col_width :]
    unit_part = solution[:, :, : super_count * col_width]
    squares = jnp.sum(unit_part * unit_part, axis=2)
    variance = taken_together(squares, COL)
    return (mean_x, variance)


def solution(mesh):
    finer = Mesh(mesh.devices.reshape(mesh.shape["row"], 8, 4), ("row", "col_0", "col_1"))
    placed = (
        P(None, "row", None, COL),
        P(None, None, "row"),
        P(None, None, "row"),
        P(),
        P(None, "row", COL),
    )
    return jax.shard_map(
        body,
        mesh=finer,
        in_specs=placed,
        out_specs=(P(None, "row", COL), P(None, "row")),
        check_vma=False,
    )
```

profile of v0, /device:TPU:8, one launch (start us, length us, event | category | flops | bytes accessed | tf_op | source)
XLA Modules:
  0.0 674.4 jit_solution(18095809335935411941)
XLA Ops:
  20.2 13.1 %all_gather.45 = f32[2,256,256]{1,0,2:T(2,128)S(1)} all-gather(f32[2,256,64]{1,0,2:T(2,128)S(1)} %pad_maximum_fusion), channel_id=1, replica_groups=mesh['row'=8,'col_0'=8,'col_1'=4] {'col_1'}, dimensions={2}, use_global_device_ids=true | all-gather | bytes 655360 | tf_op jit(solution)/shard_map/all_gather | solution.py:43
  35.0 5.7 all-to-all-start
  41.1 10.7 %broadcast_select_fusion = f32[6,2048,256]{2,1,0:T(8,128)} fusion(f32[6,2048,256]{2,1,0:T(8,128)} %param.18, pred[2048,256]{1,0:T(8,128)(4,1)S(1)} %iota_compare_fusion), kind=kLoop, calls=%fused_computation | loop fusion | flops 3145728 | bytes 25690112 | tf_op jit(solution)/shard_map/jit(_where)/select_n | solution.py:81
  55.6 36.5 %all-gather.10.cloned.1.call-done = f32[2,256,2048]{2,1,0:T(8,128)} async-done(((f32[2,256,256]{2,1,0:T(8,128)}), f32[2,256,2048]{2,1,0:T(8,128)}) %all-gather.10.cloned.1.call-update) | async-done | bytes 4194320 | tf_op jit(solution)/shard_map/all_gather | solution.py:43
  92.1 5.8 convolution_bitcast_fusion.4
  103.3 13.1 %all_gather.48 = f32[2,256,256]{1,0,2:T(2,128)S(1)} all-gather(f32[2,256,64]{1,0,2:T(2,128)S(1)} %pad_maximum_fusion.1), channel_id=1, replica_groups=mesh['row'=8,'col_0'=8,'col_1'=4] {'col_1'}, dimensions={2}, use_global_device_ids=true | all-gather | bytes 655360 | tf_op jit(solution)/shard_map/all_gather | solution.py:43
  117.6 10.2 %reduce-scatter.6.cloned.1.call-done = f32[256,66]{0,1:T(8,128)} async-done(((f32[2048,66]{0,1:T(8,128)}), f32[256,66]{0,1:T(8,128)}) %reduce-scatter.6.cloned.1.call-update) | async-done | bytes 67600 | tf_op jit(solution)/shard_map/reduce_scatter | solution.py:35
  127.9 14.5 %all_gather.47 = f32[2048,66]{0,1:T(8,128)S(1)} all-gather(f32[256,66]{0,1:T(8,128)} %reduce-scatter.6.cloned.1.call-done), channel_id=1, replica_groups=mesh['row'=8,'col_0'=8,'col_1'=4] {'row'}, dimensions={0}, use_global_device_ids=true | all-gather | bytes 608256 | tf_op jit(solution)/shard_map/all_gather | solution.py:36
  145.5 40.6 %all-gather.12.cloned.1.call-done = f32[2,256,2048]{2,1,0:T(8,128)} async-done(((f32[2,256,256]{2,1,0:T(8,128)}), f32[2,256,2048]{2,1,0:T(8,128)}) %all-gather.12.cloned.1.call-update) | async-done | bytes 4194320 | tf_op jit(solution)/shard_map/all_gather | solution.py:43
  186.1 5.7 convolution_bitcast_fusion.3
  191.9 30.6 %reduce-scatter.8.cloned.1.call-done = f32[256,130]{0,1:T(8,128)} async-done(((f32[2048,130]{0,1:T(8,128)}), f32[256,130]{0,1:T(8,128)}) %reduce-scatter.8.cloned.1.call-update) | async-done | bytes 133136 | tf_op jit(solution)/shard_map/reduce_scatter | solution.py:35
  222.7 13.2 %all_gather.51 = f32[2,256,256]{1,0,2:T(2,128)S(1)} all-gather(f32[2,256,64]{1,0,2:T(2,128)S(1)} %pad_maximum_fusion.2), channel_id=1, replica_groups=mesh['row'=8,'col_0'=8,'col_1'=4] {'col_1'}, dimensions={2}, use_global_device_ids=true | all-gather | bytes 655360 | tf_op jit(solution)/shard_map/all_gather | solution.py:43
  237.0 13.5 %all-gather.14.cloned.1.call-done = f32[2048,130]{0,1:T(8,128)} async-done(((f32[256,130]{0,1:T(8,128)}), f32[2048,130]{0,1:T(8,128)}) %all-gather.14.cloned.1.call-update) | async-done | bytes 1064976 | tf_op jit(solution)/shard_map/all_gather | solution.py:36
  255.9 52.6 %all-gather.16.cloned.1.call-done = f32[2,256,2048]{2,1,0:T(8,128)} async-done(((f32[2,256,256]{2,1,0:T(8,128)}), f32[2,256,2048]{2,1,0:T(8,128)}) %all-gather.16.cloned.1.call-update) | async-done | bytes 4194320 | tf_op jit(solution)/shard_map/all_gather | solution.py:43
  308.6 6.6 convolution_bitcast_fusion.2
  315.2 31.2 %reduce-scatter.10.cloned.1.call-done = f32[256,194]{0,1:T(8,128)} async-done(((f32[2048,194]{0,1:T(8,128)}), f32[256,194]{0,1:T(8,128)}) %reduce-scatter.10.cloned.1.call-update) | async-done | bytes 198672 | tf_op jit(solution)/shard_map/reduce_scatter | solution.py:35
  354.1 13.2 %all_gather.54 = f32[2,256,256]{1,0,2:T(2,128)S(1)} all-gather(f32[2,256,64]{1,0,2:T(2,128)S(1)} %pad_maximum_fusion.3), channel_id=1, replica_groups=mesh['row'=8,'col_0'=8,'col_1'=4] {'col_1'}, dimensions={2}, use_global_device_ids=true | all-gather | bytes 655360 | tf_op jit(solution)/shard_map/all_gather | solution.py:43
  368.7 7.0 %all-gather.18.cloned.1.call-done = f32[2048,194]{0,1:T(8,128)} async-done(((f32[256,194]{0,1:T(8,128)}), f32[2048,194]{0,1:T(8,128)}) %all-gather.18.cloned.1.call-update) | async-done | bytes 1589264 | tf_op jit(solution)/shard_map/all_gather | solution.py:36
  378.1 3.6 fusion.42
  381.8 52.3 %all-gather.20.cloned.1.call-done = f32[2,256,2048]{2,1,0:T(8,128)} async-done(((f32[2,256,256]{2,1,0:T(8,128)}), f32[2,256,2048]{2,1,0:T(8,128)}) %all-gather.20.cloned.1.call-update) | async-done | bytes 4194320 | tf_op jit(solution)/shard_map/all_gather | solution.py:43
  434.1 7.5 %convolution_bitcast_fusion.1 = f32[2048,258]{0,1:T(8,128)} fusion(f32[2,256,2048]{2,1,0:T(8,128)} %all-gather.20.cloned.1.call-done, f32[1,256,258]{1,2,0:T(8,128)S(1)} %slice_bitcast_fusion.36, f32[1,256,258]{1,2,0:T(8,128)S(1)} %slice_bitcast_fusion.37), kind=kOutput, calls=%fused_computation.9 | convolution fusion | flops 3246523392 | bytes 6836224 | tf_op jit(solution)/shard_map/tiw,tin->wn/dot_general | solution.py:53
  441.7 32.1 %reduce-scatter.12.cloned.1.call-done = f32[256,258]{0,1:T(8,128)} async-done(((f32[2048,258]{0,1:T(8,128)}), f32[256,258]{0,1:T(8,128)}) %reduce-scatter.12.cloned.1.call-update) | async-done | bytes 264208 | tf_op jit(solution)/shard_map/reduce_scatter | solution.py:35
  474.0 13.1 %all_gather.57 = f32[2,256,256]{1,0,2:T(2,128)S(1)} all-gather(f32[2,256,64]{1,0,2:T(2,128)S(1)} %pad_maximum_fusion.4), channel_id=1, replica_groups=mesh['row'=8,'col_0'=8,'col_1'=4] {'col_1'}, dimensions={2}, use_global_device_ids=true | all-gather | bytes 655360 | tf_op jit(solution)/shard_map/all_gather | solution.py:43
  488.4 16.2 %all-gather.22.cloned.1.call-done = f32[2048,258]{0,1:T(8,128)} async-done(((f32[256,258]{0,1:T(8,128)}), f32[2048,258]{0,1:T(8,128)}) %all-gather.22.cloned.1.call-update) | async-done | bytes 2113552 | tf_op jit(solution)/shard_map/all_gather | solution.py:36
  507.2 4.0 fusion.36
  512.0 50.5 %all-gather.24.cloned.1.call-done = f32[2,256,2048]{2,1,0:T(8,128)} async-done(((f32[2,256,256]{2,1,0:T(8,128)}), f32[2,256,2048]{2,1,0:T(8,128)}) %all-gather.24.cloned.1.call-update) | async-done | bytes 4194320 | tf_op jit(solution)/shard_map/all_gather | solution.py:43
  562.5 8.3 %convolution_bitcast_fusion = f32[2048,322]{0,1:T(8,128)} fusion(f32[2,256,2048]{2,1,0:T(8,128)} %all-gather.24.cloned.1.call-done, f32[1,256,322]{1,2,0:T(8,128)S(1)} %slice_bitcast_fusion.34, f32[1,256,322]{1,2,0:T(8,128)} %slice_bitcast_fusion.35), kind=kOutput, calls=%fused_computation.8 | convolution fusion | flops 4051862528 | bytes 7491584 | tf_op jit(solution)/shard_map/tiw,tin->wn/dot_general | solution.py:53
  570.9 33.1 %reduce-scatter.14.cloned.1.call-done = f32[256,322]{0,1:T(8,128)} async-done(((f32[2048,322]{0,1:T(8,128)}), f32[256,322]{0,1:T(8,128)}) %reduce-scatter.14.cloned.1.call-update) | async-done | bytes 329744 | tf_op jit(solution)/shard_map/reduce_scatter | solution.py:35
  604.0 31.8 %all-gather.26.cloned.1.call-done = f32[2048,322]{0,1:T(8,128)} async-done(((f32[256,322]{0,1:T(8,128)}), f32[2048,322]{0,1:T(8,128)}) %all-gather.26.cloned.1.call-update) | async-done | bytes 2637840 | tf_op jit(solution)/shard_map/all_gather | solution.py:36
  638.6 4.4 fusion.30
  643.8 9.8 %all-to-all-start.1 = ((f32[32,6,256]{2,1,0:T(8,128)}), f32[32,6,256]{2,1,0:T(8,128)S(1)}, u32[]{:S(2)}, u32[]{:S(2)}) async-start(f32[32,6,256]{2,1,0:T(8,128)} %broadcast_in_dim.18), calls=%async_computation.6 | async-start | bytes 524288 | tf_op jit(solution)/shard_map/all_to_all | solution.py:20
  654.3 12.8 %all-to-all-done.1 = f32[32,6,256]{2,1,0:T(8,128)S(1)} async-done(((f32[32,6,256]{2,1,0:T(8,128)}), f32[32,6,256]{2,1,0:T(8,128)S(1)}, u32[]{:S(2)}, u32[]{:S(2)}) %all-to-all-start.1) | async-done | bytes 196640 | tf_op jit(solution)/shard_map/all_to_all | solution.py:20
  (101 shorter events, 44.3 us)
Async XLA Ops:
  7.2 84.9 %all-gather.10.cloned.1.call-start = ((), (), s32[]{:S(2)}) async-start(), calls=%async_computation.7 | async-start | bytes 4718592 | tf_op jit(solution)/shard_map/all_gather | solution.py:43
  19.9 14.4 %copy-start.2 = (f32[6,256,2]{1,2,0:T(2,128)S(1)}, f32[6,256,2]{1,2,0:T(2,128)}, u32[]{:S(2)}) copy-start(f32[6,256,2]{1,2,0:T(2,128)} %param.21) | copy-start | bytes 36868
  35.0 16.9 %all-to-all-start = ((f32[8,6,256,2]{2,3,1,0:T(2,128)}), f32[8,6,256,2]{2,3,1,0:T(2,128)S(1)}, u32[]{:S(2)}, u32[]{:S(2)}) async-start(f32[8,6,256,2]{2,3,1,0:T(2,128)} %broadcast_in_dim.16), calls=%async_computation | async-start | bytes 196608 | tf_op jit(solution)/shard_map/all_to_all | solution.py:20
  40.7 87.1 %reduce-scatter.6.cloned.1.call-start = ((), (), s32[]{:S(2)}) async-start(), calls=%async_computation.8 | async-start | bytes 663552 | tf_op jit(solution)/shard_map/reduce_scatter | solution.py:35
  97.9 88.3 %all-gather.12.cloned.1.call-start = ((), (), s32[]{:S(2)}) async-start(), calls=%async_computation.9 | async-start | bytes 4718592 | tf_op jit(solution)/shard_map/all_gather | solution.py:43
  117.4 105.1 %reduce-scatter.8.cloned.1.call-start = ((), (), s32[]{:S(2)}) async-start(), calls=%async_computation.10 | async-start | bytes 1253376 | tf_op jit(solution)/shard_map/reduce_scatter | solution.py:35
  191.9 58.6 %all-gather.14.cloned.1.call-start = ((), (), s32[]{:S(2)}) async-start(), calls=%async_computation.11 | async-start | bytes 1253376 | tf_op jit(solution)/shard_map/all_gather | solution.py:36
  222.5 86.1 %all-gather.16.cloned.1.call-start = ((), (), s32[]{:S(2)}) async-start(), calls=%async_computation.12 | async-start | bytes 4718592 | tf_op jit(solution)/shard_map/all_gather | solution.py:43
  236.9 109.5 %reduce-scatter.10.cloned.1.call-start = ((), (), s32[]{:S(2)}) async-start(), calls=%async_computation.13 | async-start | bytes 1843200 | tf_op jit(solution)/shard_map/reduce_scatter | solution.py:35
  315.2 60.5 %all-gather.18.cloned.1.call-start = ((), (), s32[]{:S(2)}) async-start(), calls=%async_computation.14 | async-start | bytes 1843200 | tf_op jit(solution)/shard_map/all_gather | solution.py:36
  346.5 87.6 %all-gather.20.cloned.1.call-start = ((), (), s32[]{:S(2)}) async-start(), calls=%async_computation.15 | async-start | bytes 4718592 | tf_op jit(solution)/shard_map/all_gather | solution.py:43
  368.5 105.3 %reduce-scatter.12.cloned.1.call-start = ((), (), s32[]{:S(2)}) async-start(), calls=%async_computation.16 | async-start | bytes 2433024 | tf_op jit(solution)/shard_map/reduce_scatter | solution.py:35
  441.6 32.2 %copy-start = (f32[1,256,64]{1,0,2:T(1,128)S(1)}, f32[1,256,64]{1,0,2:T(1,128)}, u32[]{:S(2)}) copy-start(f32[1,256,64]{1,0,2:T(1,128)} %get-tuple-element.88) | copy-start | bytes 196612
  441.6 63.0 %copy-start.1 = (f32[1,8,256,2]{2,3,0,1:T(2,128)S(1)}, f32[1,8,256,2]{2,3,0,1:T(2,128)}, u32[]{:S(2)}) copy-start(f32[1,8,256,2]{2,3,0,1:T(2,128)} %get-tuple-element.98) | copy-start | bytes 49156
  441.6 62.9 %all-gather.22.cloned.1.call-start = ((), (), s32[]{:S(2)}) async-start(), calls=%async_computation.17 | async-start | bytes 2433024 | tf_op jit(solution)/shard_map/all_gather | solution.py:36
  473.8 88.7 %all-gather.24.cloned.1.call-start = ((), (), s32[]{:S(2)}) async-start(), calls=%async_computation.18 | async-start | bytes 4718592 | tf_op jit(solution)/shard_map/all_gather | solution.py:43
  488.1 115.9 %reduce-scatter.14.cloned.1.call-start = ((), (), s32[]{:S(2)}) async-start(), calls=%async_computation.19 | async-start | bytes 3022848 | tf_op jit(solution)/shard_map/reduce_scatter | solution.py:35
  570.9 64.9 %all-gather.26.cloned.1.call-start = ((), (), s32[]{:S(2)}) async-start(), calls=%async_computation.20 | async-start | bytes 3022848 | tf_op jit(solution)/shard_map/all_gather | solution.py:36
  643.8 23.2 %all-to-all-start.1 = ((f32[32,6,256]{2,1,0:T(8,128)}), f32[32,6,256]{2,1,0:T(8,128)S(1)}, u32[]{:S(2)}, u32[]{:S(2)}) async-start(f32[32,6,256]{2,1,0:T(8,128)} %broadcast_in_dim.18), calls=%async_computation.6 | async-start | bytes 524288 | tf_op jit(solution)/shard_map/all_to_all | solution.py:20
Sparse Core Ops, SparseCore 0:
  34.5 57.5 all-gather.9
  98.0 29.8 reduce-scatter.5
  129.7 56.4 all-gather.11
  192.0 30.4 reduce-scatter.7
  224.2 26.2 all-gather.13
  252.1 56.4 all-gather.15
  315.3 31.1 reduce-scatter.9
  348.3 27.3 all-gather.17
  377.5 56.5 all-gather.19
  441.7 31.9 reduce-scatter.11
  475.6 28.8 all-gather.21
  506.2 56.2 all-gather.23
  571.0 32.9 reduce-scatter.13
  605.7 30.0 all-gather.25
where the time goes:
time: 683 us; the launch traced here: 674 us
  waiting for transfers between devices  451 us (66%)
  blocking collectives  80.2 us (12%)
  matrix products  54.9 us (8%)
  other arithmetic  32 us (5%)
  between operations  26.9 us (4%)
  starting transfers between devices  16.5 us (2%)
  local copies, waits for them, and re-layouts  12.8 us (2%)
    all_gather x5, waiting for transfers between devices, gathered_by_axis(): nearer = lax.all_gather(array, axes[-1], axis=dim, tiled=True)  233 us
    reduce_scatter x5, waiting for transfers between devices, total_of(): own = lax.psum_scatter(padded, axis, scatter_dimension=0, tiled=True)  137 us
    all_gather x4, waiting for transfers between devices, total_of(): whole = lax.all_gather(own, axis, axis=0, tiled=True)  68.4 us
    all_gather x5, blocking collectives, gathered_by_axis(): nearer = lax.all_gather(array, axes[-1], axis=dim, tiled=True)  65.7 us
    dot_general x5, matrix products, contract(): return jnp.einsum('tiw,tin->wn', panel_piece, selected, precision=HIGHEST)  33.9 us
    dot_general x6, matrix products, body(): jnp.dot(lower_inv[current_sup].T, right, precision=HIGHEST, preferred_ele...  21 us
    all_to_all x2, starting transfers between devices, from_everyone(): return lax.all_to_all(copies, axis, split_axis=0, concat_axis=0, tiled=True)  15.5 us
    all_gather x1, blocking collectives, total_of(): whole = lax.all_gather(own, axis, axis=0, tiled=True)  14.5 us
  transfers between devices with their start and end apart: 16, of which 15 were waited for; matrix products, arithmetic and copies ran while one was open for 7% of the time, Pallas kernels for 0%

commit v1 on v0

--- a/solution.py
+++ b/solution.py
@@ -33,7 +33,8 @@
     lines = array.reshape(-1, *array.shape[1:][-1:])
     padded = filled_up(lines, lax.axis_size(axis))
     own = lax.psum_scatter(padded, axis, scatter_dimension=0, tiled=True)
-    whole = lax.all_gather(own, axis, axis=0, tiled=True)
+    sent = jnp.stack([own] * lax.axis_size(axis))
+    whole = jnp.concatenate(lax.all_to_all(sent, axis, 0, 0), axis=0)
     return whole[: len(lines)].reshape(array.shape)
 
 

time: 683 us -> 603 us (0.88)
  waiting for transfers between devices: 451 us -> 252 us
  blocking collectives: 80.2 us -> 186 us
  local copies, waits for them, and re-layouts: 12.8 us -> 26.4 us
  other arithmetic: 32 us -> 24.4 us
    all_to_all x0 -> x4, blocking collectives: none -> 120 us  [total_of(): whole = jnp.concatenate(lax.all_to_all(sent, axis, 0, 0), axis=0)]
    all_gather x5, waiting for transfers between devices: 233 us -> 147 us  [gathered_by_axis(): nearer = lax.all_gather(array, axes[-1], axis=dim, tiled=True)]
    all_gather x4 -> x0, waiting for transfers between devices: 68.4 us -> none  [total_of(): whole = lax.all_gather(own, axis, axis=0, tiled=True)]
    reduce_scatter x5, waiting for transfers between devices: 137 us -> 85.1 us  [total_of(): own = lax.psum_scatter(padded, axis, scatter_dimension=0, tiled=True)]
    all_gather x1 -> x0, blocking collectives: 14.5 us -> none  [total_of(): whole = lax.all_gather(own, axis, axis=0, tiled=True)]
    all_to_all x0 -> x1, waiting for transfers between devices: none -> 8.35 us  [total_of(): whole = jnp.concatenate(lax.all_to_all(sent, axis, 0, 0), axis=0)]
    all_to_all x0 -> x1, starting transfers between devices: none -> 6.96 us  [total_of(): whole = jnp.concatenate(lax.all_to_all(sent, axis, 0, 0), axis=0)]
  transfers between devices with their start and end apart: 16 -> 13, of which waited for: 15 -> 12; matrix products, arithmetic and copies ran while one was open for 7% -> 8% of each run, Pallas kernels for 0% -> 0%
where the time goes in v1:
time: 603 us; the launch traced here: 595 us
  waiting for transfers between devices  252 us (42%)
  blocking collectives  186 us (31%)
  matrix products  55.1 us (9%)
  between operations  27.6 us (5%)
  local copies, waits for them, and re-layouts  26.4 us (4%)
  other arithmetic  24.4 us (4%)
  starting transfers between devices  23 us (4%)
    all_gather x5, waiting for transfers between devices, gathered_by_axis(): nearer = lax.all_gather(array, axes[-1], axis=dim, tiled=True)  147 us
    all_to_all x4, blocking collectives, total_of(): whole = jnp.concatenate(lax.all_to_all(sent, axis, 0, 0), axis=0)  120 us
    reduce_scatter x5, waiting for transfers between devices, total_of(): own = lax.psum_scatter(padded, axis, scatter_dimension=0, tiled=True)  85.1 us
    all_gather x5, blocking collectives, gathered_by_axis(): nearer = lax.all_gather(array, axes[-1], axis=dim, tiled=True)  65.7 us
    dot_general x5, matrix products, contract(): return jnp.einsum('tiw,tin->wn', panel_piece, selected, precision=HIGHEST)  34 us
    dot_general x6, matrix products, body(): jnp.dot(lower_inv[current_sup].T, right, precision=HIGHEST, preferred_ele...  21.1 us
    all_to_all x2, starting transfers between devices, from_everyone(): return lax.all_to_all(copies, axis, split_axis=0, concat_axis=0, tiled=True)  15.5 us
  transfers between devices with their start and end apart: 13, of which 12 were waited for; matrix products, arithmetic and copies ran while one was open for 8% of the time, Pallas kernels for 0%

profile of v1, /device:TPU:8, one launch (start us, length us, event | category | flops | bytes accessed | tf_op | source)
XLA Modules:
  0.0 595.0 jit_solution(18023636908558563428)
XLA Ops:
  20.2 13.1 %all_gather.30 = f32[2,256,256]{1,0,2:T(2,128)S(1)} all-gather(f32[2,256,64]{1,0,2:T(2,128)S(1)} %pad_maximum_fusion), channel_id=1, replica_groups=mesh['row'=8,'col_0'=8,'col_1'=4] {'col_1'}, dimensions={2}, use_global_device_ids=true | all-gather | bytes 655360 | tf_op jit(solution)/shard_map/all_gather | solution.py:44
  35.1 5.7 all-to-all-start
  41.2 10.7 %broadcast_select_fusion = f32[6,2048,256]{2,1,0:T(8,128)} fusion(f32[6,2048,256]{2,1,0:T(8,128)} %param.18, pred[2048,256]{1,0:T(8,128)(4,1)S(1)} %iota_compare_fusion), kind=kLoop, calls=%fused_computation | loop fusion | flops 3145728 | bytes 25690112 | tf_op jit(solution)/shard_map/jit(_where)/select_n | solution.py:82
  55.7 36.5 %all-gather.6.cloned.1.call-done = f32[2,256,2048]{2,1,0:T(8,128)} async-done(((f32[2,256,256]{2,1,0:T(8,128)}), f32[2,256,2048]{2,1,0:T(8,128)}) %all-gather.6.cloned.1.call-update) | async-done | bytes 4194320 | tf_op jit(solution)/shard_map/all_gather | solution.py:44
  92.1 5.8 convolution_bitcast_fusion.4
  104.3 13.1 %all_gather.32 = f32[2,256,256]{1,0,2:T(2,128)S(1)} all-gather(f32[2,256,64]{1,0,2:T(2,128)S(1)} %pad_maximum_fusion.1), channel_id=1, replica_groups=mesh['row'=8,'col_0'=8,'col_1'=4] {'col_1'}, dimensions={2}, use_global_device_ids=true | all-gather | bytes 655360 | tf_op jit(solution)/shard_map/all_gather | solution.py:44
  118.4 9.6 %reduce-scatter.6.cloned.1.call-done = f32[256,66]{0,1:T(8,128)} async-done(((f32[2048,66]{0,1:T(8,128)}), f32[256,66]{0,1:T(8,128)}) %reduce-scatter.6.cloned.1.call-update) | async-done | bytes 67600 | tf_op jit(solution)/shard_map/reduce_scatter | solution.py:35
  129.7 7.0 %all-to-all-start.1 = ((f32[8,256,66]{1,2,0:T(8,128)}), f32[8,256,66]{1,2,0:T(8,128)S(1)}, u32[]{:S(2)}, u32[]{:S(2)}) async-start(f32[8,256,66]{1,2,0:T(8,128)} %stack.54), calls=%async_computation.2 | async-start | bytes 1179648 | tf_op jit(solution)/shard_map/all_to_all | solution.py:37
  137.9 8.4 %all-to-all-done.1 = f32[8,256,66]{1,2,0:T(8,128)S(1)} async-done(((f32[8,256,66]{1,2,0:T(8,128)}), f32[8,256,66]{1,2,0:T(8,128)S(1)}, u32[]{:S(2)}, u32[]{:S(2)}) %all-to-all-start.1) | async-done | bytes 540704 | tf_op jit(solution)/shard_map/all_to_all | solution.py:37
  150.1 36.1 %all-gather.8.cloned.1.call-done = f32[2,256,2048]{2,1,0:T(8,128)} async-done(((f32[2,256,256]{2,1,0:T(8,128)}), f32[2,256,2048]{2,1,0:T(8,128)}) %all-gather.8.cloned.1.call-update) | async-done | bytes 4194320 | tf_op jit(solution)/shard_map/all_gather | solution.py:44
  186.2 5.7 convolution_bitcast_fusion.3
  192.1 13.1 %all_gather.34 = f32[2,256,256]{1,0,2:T(2,128)S(1)} all-gather(f32[2,256,64]{1,0,2:T(2,128)S(1)} %pad_maximum_fusion.2), channel_id=1, replica_groups=mesh['row'=8,'col_0'=8,'col_1'=4] {'col_1'}, dimensions={2}, use_global_device_ids=true | all-gather | bytes 655360 | tf_op jit(solution)/shard_map/all_gather | solution.py:44
  206.3 16.3 %reduce-scatter.8.cloned.1.call-done = f32[256,130]{0,1:T(8,128)} async-done(((f32[2048,130]{0,1:T(8,128)}), f32[256,130]{0,1:T(8,128)}) %reduce-scatter.8.cloned.1.call-update) | async-done | bytes 133136 | tf_op jit(solution)/shard_map/reduce_scatter | solution.py:35
  223.5 21.3 %all_to_all.35 = f32[8,256,130]{1,2,0:T(8,128)S(1)} all-to-all(f32[8,256,130]{1,2,0:T(8,128)S(1)} %stack.59), channel_id=1, replica_groups=mesh['row'=8,'col_0'=8,'col_1'=4] {'row'}, dimensions={0} | all-to-all | bytes 2129920 | tf_op jit(solution)/shard_map/all_to_all | solution.py:37
  249.1 31.7 %all-gather.10.cloned.1.call-done = f32[2,256,2048]{2,1,0:T(8,128)} async-done(((f32[2,256,256]{2,1,0:T(8,128)}), f32[2,256,2048]{2,1,0:T(8,128)}) %all-gather.10.cloned.1.call-update) | async-done | bytes 4194320 | tf_op jit(solution)/shard_map/all_gather | solution.py:44
  280.8 6.6 %convolution_bitcast_fusion.2 = f32[2048,194]{0,1:T(8,128)} fusion(f32[2,256,2048]{2,1,0:T(8,128)} %all-gather.10.cloned.1.call-done, f32[1,256,194]{1,2,0:T(8,128)S(1)} %slice_bitcast_fusion.38, f32[1,256,194]{1,2,0:T(8,128)S(1)} %slice_bitcast_fusion.39), kind=kOutput, calls=%fused_computation.18 | convolution fusion | flops 2441184256 | bytes 6180864 | tf_op jit(solution)/shard_map/tiw,tin->wn/dot_general | solution.py:54
  295.2 13.3 %all_gather.36 = f32[2,256,256]{1,0,2:T(2,128)S(1)} all-gather(f32[2,256,64]{1,0,2:T(2,128)S(1)} %pad_maximum_fusion.3), channel_id=1, replica_groups=mesh['row'=8,'col_0'=8,'col_1'=4] {'col_1'}, dimensions={2}, use_global_device_ids=true | all-gather | bytes 655360 | tf_op jit(solution)/shard_map/all_gather | solution.py:44
  309.6 9.2 %reduce-scatter.10.cloned.1.call-done = f32[256,194]{0,1:T(8,128)} async-done(((f32[2048,194]{0,1:T(8,128)}), f32[256,194]{0,1:T(8,128)}) %reduce-scatter.10.cloned.1.call-update) | async-done | bytes 198672 | tf_op jit(solution)/shard_map/reduce_scatter | solution.py:35
  319.8 27.1 %all_to_all.36 = f32[8,256,194]{1,2,0:T(8,128)S(1)} all-to-all(f32[8,256,194]{1,2,0:T(8,128)S(1)} %stack.64), channel_id=1, replica_groups=mesh['row'=8,'col_0'=8,'col_1'=4] {'row'}, dimensions={0} | all-to-all | bytes 3178496 | tf_op jit(solution)/shard_map/all_to_all | solution.py:37
  352.1 25.2 %all-gather.12.cloned.1.call-done = f32[2,256,2048]{2,1,0:T(8,128)} async-done(((f32[2,256,256]{2,1,0:T(8,128)}), f32[2,256,2048]{2,1,0:T(8,128)}) %all-gather.12.cloned.1.call-update) | async-done | bytes 4194320 | tf_op jit(solution)/shard_map/all_gather | solution.py:44
  377.3 7.5 %convolution_bitcast_fusion.1 = f32[2048,258]{0,1:T(8,128)} fusion(f32[2,256,2048]{2,1,0:T(8,128)} %all-gather.12.cloned.1.call-done, f32[1,256,258]{1,2,0:T(8,128)S(1)} %slice_bitcast_fusion.36, f32[1,256,258]{1,2,0:T(8,128)S(1)} %slice_bitcast_fusion.37), kind=kOutput, calls=%fused_computation.9 | convolution fusion | flops 3246523392 | bytes 6836224 | tf_op jit(solution)/shard_map/tiw,tin->wn/dot_general | solution.py:54
  385.8 13.1 %all_gather.38 = f32[2,256,256]{1,0,2:T(2,128)S(1)} all-gather(f32[2,256,64]{1,0,2:T(2,128)S(1)} %pad_maximum_fusion.4), channel_id=1, replica_groups=mesh['row'=8,'col_0'=8,'col_1'=4] {'col_1'}, dimensions={2}, use_global_device_ids=true | all-gather | bytes 655360 | tf_op jit(solution)/shard_map/all_gather | solution.py:44
  400.0 17.0 %reduce-scatter.12.cloned.1.call-done = f32[256,258]{0,1:T(8,128)} async-done(((f32[2048,258]{0,1:T(8,128)}), f32[256,258]{0,1:T(8,128)}) %reduce-scatter.12.cloned.1.call-update) | async-done | bytes 264208 | tf_op jit(solution)/shard_map/reduce_scatter | solution.py:35
  418.1 33.3 %all_to_all.37 = f32[8,256,258]{1,2,0:T(8,128)S(1)} all-to-all(f32[8,256,258]{1,2,0:T(8,128)S(1)} %stack.69), channel_id=1, replica_groups=mesh['row'=8,'col_0'=8,'col_1'=4] {'row'}, dimensions={0} | all-to-all | bytes 4227072 | tf_op jit(solution)/shard_map/all_to_all | solution.py:37
  453.4 4.0 fusion.36
  458.3 17.3 %all-gather.14.cloned.1.call-done = f32[2,256,2048]{2,1,0:T(8,128)} async-done(((f32[2,256,256]{2,1,0:T(8,128)}), f32[2,256,2048]{2,1,0:T(8,128)}) %all-gather.14.cloned.1.call-update) | async-done | bytes 4194320 | tf_op jit(solution)/shard_map/all_gather | solution.py:44
  475.6 8.4 %convolution_bitcast_fusion = f32[2048,322]{0,1:T(8,128)} fusion(f32[2,256,2048]{2,1,0:T(8,128)} %all-gather.14.cloned.1.call-done, f32[1,256,322]{1,2,0:T(8,128)S(1)} %slice_bitcast_fusion.34, f32[1,256,322]{1,2,0:T(8,128)} %slice_bitcast_fusion.35), kind=kOutput, calls=%fused_computation.8 | convolution fusion | flops 4051862528 | bytes 7491584 | tf_op jit(solution)/shard_map/tiw,tin->wn/dot_general | solution.py:54
  483.9 33.1 %reduce-scatter.14.cloned.1.call-done = f32[256,322]{0,1:T(8,128)} async-done(((f32[2048,322]{0,1:T(8,128)}), f32[256,322]{0,1:T(8,128)}) %reduce-scatter.14.cloned.1.call-update) | async-done | bytes 329744 | tf_op jit(solution)/shard_map/reduce_scatter | solution.py:35
  518.2 38.8 %all_to_all.38 = f32[8,256,322]{1,2,0:T(8,128)S(1)} all-to-all(f32[8,256,322]{1,2,0:T(8,128)S(1)} %stack.74), channel_id=1, replica_groups=mesh['row'=8,'col_0'=8,'col_1'=4] {'row'}, dimensions={0} | all-to-all | bytes 5275648 | tf_op jit(solution)/shard_map/all_to_all | solution.py:37
  559.6 4.4 fusion.30
  564.9 9.8 %all-to-all-start.6 = ((f32[32,6,256]{2,1,0:T(8,128)}), f32[32,6,256]{2,1,0:T(8,128)S(1)}, u32[]{:S(2)}, u32[]{:S(2)}) async-start(f32[32,6,256]{2,1,0:T(8,128)} %broadcast_in_dim.18), calls=%async_computation.11 | async-start | bytes 524288 | tf_op jit(solution)/shard_map/all_to_all | solution.py:20
  575.3 12.0 %all-to-all-done.6 = f32[32,6,256]{2,1,0:T(8,128)S(1)} async-done(((f32[32,6,256]{2,1,0:T(8,128)}), f32[32,6,256]{2,1,0:T(8,128)S(1)}, u32[]{:S(2)}, u32[]{:S(2)}) %all-to-all-start.6) | async-done | bytes 196640 | tf_op jit(solution)/shard_map/all_to_all | solution.py:20
  (122 shorter events, 53.5 us)
Async XLA Ops:
  7.2 85.0 %all-gather.6.cloned.1.call-start = ((), (), s32[]{:S(2)}) async-start(), calls=%async_computation.12 | async-start | bytes 4718592 | tf_op jit(solution)/shard_map/all_gather | solution.py:44
  20.0 14.4 %copy-start.6 = (f32[6,256,2]{1,2,0:T(2,128)S(1)}, f32[6,256,2]{1,2,0:T(2,128)}, u32[]{:S(2)}) copy-start(f32[6,256,2]{1,2,0:T(2,128)} %param.21) | copy-start | bytes 36868
  35.1 16.9 %all-to-all-start = ((f32[8,6,256,2]{2,3,1,0:T(2,128)}), f32[8,6,256,2]{2,3,1,0:T(2,128)S(1)}, u32[]{:S(2)}, u32[]{:S(2)}) async-start(f32[8,6,256,2]{2,3,1,0:T(2,128)} %broadcast_in_dim.16), calls=%async_computation | async-start | bytes 196608 | tf_op jit(solution)/shard_map/all_to_all | solution.py:20
  40.8 87.2 %reduce-scatter.6.cloned.1.call-start = ((), (), s32[]{:S(2)}) async-start(), calls=%async_computation.13 | async-start | bytes 663552 | tf_op jit(solution)/shard_map/reduce_scatter | solution.py:35
  55.5 42.4 %copy-start = (f32[1,256,66]{1,2,0:T(8,128)}, f32[1,256,66]{1,2,0:T(8,128)S(1)}, u32[]{:S(2)}) copy-start(f32[1,256,66]{1,2,0:T(8,128)S(1)} %fusion.53) | copy-start | bytes 202756
  98.0 88.2 %all-gather.8.cloned.1.call-start = ((), (), s32[]{:S(2)}) async-start(), calls=%async_computation.14 | async-start | bytes 4718592 | tf_op jit(solution)/shard_map/all_gather | solution.py:44
  129.7 16.5 %all-to-all-start.1 = ((f32[8,256,66]{1,2,0:T(8,128)}), f32[8,256,66]{1,2,0:T(8,128)S(1)}, u32[]{:S(2)}, u32[]{:S(2)}) async-start(f32[8,256,66]{1,2,0:T(8,128)} %stack.54), calls=%async_computation.2 | async-start | bytes 1179648 | tf_op jit(solution)/shard_map/all_to_all | solution.py:37
  136.7 85.9 %reduce-scatter.8.cloned.1.call-start = ((), (), s32[]{:S(2)}) async-start(), calls=%async_computation.15 | async-start | bytes 1253376 | tf_op jit(solution)/shard_map/reduce_scatter | solution.py:35
  146.3 0.7 copy-start.5
  150.1 41.9 %copy-start.1 = (f32[1,256,64]{1,0,2:T(1,128)S(1)}, f32[1,256,64]{1,0,2:T(1,128)}, u32[]{:S(2)}) copy-start(f32[1,256,64]{1,0,2:T(1,128)} %get-tuple-element.91) | copy-start | bytes 196612
  150.1 41.9 %copy-start.2 = (f32[1,256,64]{1,0,2:T(1,128)S(1)}, f32[1,256,64]{1,0,2:T(1,128)}, u32[]{:S(2)}) copy-start(f32[1,256,64]{1,0,2:T(1,128)} %get-tuple-element.92) | copy-start | bytes 196612
  191.9 88.9 %all-gather.10.cloned.1.call-start = ((), (), s32[]{:S(2)}) async-start(), calls=%async_computation.16 | async-start | bytes 4718592 | tf_op jit(solution)/shard_map/all_gather | solution.py:44
  206.3 112.5 %reduce-scatter.10.cloned.1.call-start = ((), (), s32[]{:S(2)}) async-start(), calls=%async_computation.17 | async-start | bytes 1843200 | tf_op jit(solution)/shard_map/reduce_scatter | solution.py:35
  287.5 89.8 %all-gather.12.cloned.1.call-start = ((), (), s32[]{:S(2)}) async-start(), calls=%async_computation.18 | async-start | bytes 4718592 | tf_op jit(solution)/shard_map/all_gather | solution.py:44
  309.5 107.5 %reduce-scatter.12.cloned.1.call-start = ((), (), s32[]{:S(2)}) async-start(), calls=%async_computation.19 | async-start | bytes 2433024 | tf_op jit(solution)/shard_map/reduce_scatter | solution.py:35
  347.5 0.7 copy-start.4
  384.8 90.7 %all-gather.14.cloned.1.call-start = ((), (), s32[]{:S(2)}) async-start(), calls=%async_computation.20 | async-start | bytes 4718592 | tf_op jit(solution)/shard_map/all_gather | solution.py:44
  400.0 117.1 %reduce-scatter.14.cloned.1.call-start = ((), (), s32[]{:S(2)}) async-start(), calls=%async_computation.21 | async-start | bytes 3022848 | tf_op jit(solution)/shard_map/reduce_scatter | solution.py:35
  452.2 0.9 copy-start.3
  564.9 22.4 %all-to-all-start.6 = ((f32[32,6,256]{2,1,0:T(8,128)}), f32[32,6,256]{2,1,0:T(8,128)S(1)}, u32[]{:S(2)}, u32[]{:S(2)}) async-start(f32[32,6,256]{2,1,0:T(8,128)} %broadcast_in_dim.18), calls=%async_computation.11 | async-start | bytes 524288 | tf_op jit(solution)/shard_map/all_to_all | solution.py:20
Sparse Core Ops, SparseCore 0:
  34.5 57.5 all-gather.5
  98.1 29.8 reduce-scatter.5
  129.8 56.3 all-gather.7
  192.0 30.4 reduce-scatter.7
  224.2 56.5 all-gather.9
  287.6 31.1 reduce-scatter.9
  320.5 56.7 all-gather.11
  384.9 32.0 reduce-scatter.11
  418.8 56.7 all-gather.13
  484.1 32.9 reduce-scatter.13
